TPU v7x, 32 devices: a whole 2x2x4 slice. The times are simulated.
32 devices in a mesh: row: 8 (over z, core), col: 4 (over y, x).
Axes of the slice: x: 2, y: 2, z: 4, core: 2. Of those that a mesh axis runs over, the one named last changes fastest.
Arguments:
- pair_exchange: bfloat16 [64, 16, 1024], P(('row', 'col')), may hold values from -6 to 6
- conduction: bfloat16 [64, 4, 1024], P(('row', 'col')), may hold values from -6 to 6
- valence: bfloat16 [64, 4, 1024], P(('row', 'col')), may hold values from -6 to 6
- coulomb: float32 [1024], replicated, may hold values from 0.5 to 5
- screening: float32 [34, 1024], replicated, may hold values from 0.1 to 1
- energies: float32 [64, 16], P(('row', 'col')), may hold values from 1 to 9
- vectors: bfloat16 [64, 512], P(('row', 'col')), may hold values from -6 to 6
- k_coords: int32 [64, 2], P(('row', 'col')), may hold values from 0 to 31, as said below
Outputs:
- residual_block: float32 [64, 512], P(('row', 'col'))
- alpha: float32 [32, 32], replicated
Inputs may be any that keep to these rules, and one draw needn't show every extreme that they name: `k_coords`: each row holds a k-point's coordinates on the periodic 32 x 2 mesh, first then second; every mesh point occurs exactly once.
All inputs are finite; a program needn't handle non-finite values.
Results may differ from a plain program's by a relative error of at most 0.0028.
Values may be sent and summed in bfloat16 or wider, within the bound.
A program may use at most 64 MiB of HBM per device.

v0:
```python
import jax
import jax.numpy as jnp
from jax import lax
from jax.sharding import PartitionSpec as P

MX = 32
highest = lax.Precision.HIGHEST


def pair_factors(conduction, valence):
    count, valence_count, plane_count = valence.shape
    joined = (
        valence.astype(jnp.float32)[:, :, None, :] * conduction.astype(jnp.float32)[:, None, :, :]
    )
    return joined.reshape(count, valence_count * conduction.shape[1], plane_count).astype(
        jnp.bfloat16
    )


def transfer_index(rows_at, cols_at, mesh_cols):
    delta_first = jnp.mod(rows_at[:, None, 0] - cols_at[None, :, 0], MX)
    delta_second = jnp.mod(rows_at[:, None, 1] - cols_at[None, :, 1], mesh_cols)
    fold_first = jnp.minimum(delta_first, MX - delta_first)
    fold_second = jnp.minimum(delta_second, mesh_cols - delta_second)
    return (fold_first * (mesh_cols // 2 + 1) + fold_second).astype(jnp.int32)


def on_device(pair_exchange, conduction, valence, coulomb, screening, energies, vectors, k_coords):
    local_count, band_count, plane_count = pair_exchange.shape
    vector_count = vectors.shape[1] // band_count
    row_count = lax.axis_size("row")
    col_count = lax.axis_size("col")
    total_count = local_count * row_count * col_count
    mesh_cols = total_count // MX
    moving = vectors.reshape(local_count, band_count, vector_count)
    partial_density = jnp.einsum(
        "ktg,ktn->gn", pair_exchange, moving, preferred_element_type=jnp.float32
    )
    density = lax.psum(partial_density, ("row", "col"))
    block_size = 128
    sweeps = plane_count // block_size
    col_cond, col_val, col_vec, col_at = (
        lax.all_gather(conduction, "row", axis=0, tiled=True),
        lax.all_gather(valence, "row", axis=0, tiled=True),
        lax.all_gather(vectors, "row", axis=0, tiled=True),
        lax.all_gather(k_coords, "row", axis=0, tiled=True),
    )
    row_cond, row_val, row_at = (
        lax.all_gather(conduction, "col", axis=0, tiled=True),
        lax.all_gather(valence, "col", axis=0, tiled=True),
        lax.all_gather(k_coords, "col", axis=0, tiled=True),
    )
    row_pairs = pair_factors(row_cond, row_val)
    col_pairs = pair_factors(col_cond, col_val)
    indices = transfer_index(row_at, col_at, mesh_cols)
    col_moving = col_vec.reshape(-1, band_count, vector_count)

    def square_sweep(sweep_index, running):
        anchor = sweep_index * block_size
        coupling = jnp.take(
            lax.dynamic_slice_in_dim(screening, anchor, block_size, 1), indices, axis=0
        )
        row_block = lax.dynamic_slice_in_dim(row_pairs, anchor, block_size, 2)
        col_block = lax.dynamic_slice_in_dim(col_pairs, anchor, block_size, 2)
        col_proj = jnp.einsum(
            "ktg,ktn->kng", col_block, col_moving, preferred_element_type=jnp.float32
        )
        potential = jnp.einsum("ijg,jng->ing", coupling, col_proj, precision=highest)
        return running + jnp.einsum(
            "ktg,kng->ktn", row_block.astype(jnp.float32), potential, precision=highest
        )

    forward = lax.fori_loop(
        0,
        sweeps,
        square_sweep,
        jnp.zeros((row_pairs.shape[0], band_count, vector_count), jnp.float32),
    )
    owned = lax.psum_scatter(
        forward.reshape(col_count, local_count, band_count, vector_count),
        "col",
        scatter_dimension=0,
        tiled=True,
    )[0]
    moving_wide = moving.astype(jnp.float32)
    exchange_term = jnp.einsum(
        "ktg,gn->ktn", pair_exchange.astype(jnp.float32) * coulomb, density, precision=highest
    )
    applied = (
        energies[:, :, None] * moving_wide
        + 2.0 / (total_count * band_count) * exchange_term
        - owned / total_count
    )
    gram = jnp.einsum("ktm,ktn->mn", moving_wide, applied, precision=highest)
    alpha = lax.psum(gram, ("row", "col")) / (total_count * band_count)
    residual = applied - jnp.einsum("ktm,mn->ktn", moving_wide, alpha, precision=highest)
    return (residual.reshape(local_count, band_count * vector_count), alpha)


def solution(mesh):
    in_specs = (
        P(("row", "col"), None, None),
        P(("row", "col"), None, None),
        P(("row", "col"), None, None),
        P(),
        P(),
        P(("row", "col"), None),
        P(("row", "col"), None),
        P(("row", "col"), None),
    )
    out_specs = (P(("row", "col"), None), P())
    return jax.shard_map(
        on_device, mesh=mesh, in_specs=in_specs, out_specs=out_specs, check_vma=False
    )
```

profile of v0, /device:TPU:0, one launch (start us, length us, event | category | flops | bytes accessed | tf_op | source)
XLA Modules:
  0.0 299.9 jit_solution(13418184121838847277)
XLA Ops:
  8.7 13.5 %all-gather.2 = s32[8,2,2]{2,1,0:T(2,128)S(1)} all-gather(s32[1,2,2]{2,1,0:T(2,128)S(1)} %bitcast.65), channel_id=1, replica_groups=mesh['row'=8,'col'=4] {'row'}, dimensions={0}, use_global_device_ids=true | all-gather | bytes 144 | tf_op jit(solution)/shard_map/all_gather | solution.py:46
  22.1 8.1 %all-gather.1 = s32[4,2,2]{2,1,0:T(2,128)S(1)} all-gather(s32[1,2,2]{2,1,0:T(2,128)S(1)} %bitcast.66), channel_id=1, replica_groups=mesh['row'=8,'col'=4] {'col'}, dimensions={0}, use_global_device_ids=true | all-gather | bytes 80 | tf_op jit(solution)/shard_map/all_gather | solution.py:51
  30.2 14.3 %all_gather.23 = bf16[16,4,1024]{2,1,0:T(4,128)(2,1)S(1)} all-gather(bf16[2,4,1024]{2,1,0:T(4,128)(2,1)} %param.12), channel_id=1, replica_groups=mesh['row'=8,'col'=4] {'row'}, dimensions={0}, use_global_device_ids=true | all-gather | bytes 147456 | tf_op jit(solution)/shard_map/all_gather | solution.py:44
  44.5 8.3 %all_gather.21 = bf16[8,4,1024]{2,1,0:T(4,128)(2,1)S(1)} all-gather(bf16[2,4,1024]{2,1,0:T(4,128)(2,1)S(1)} %copy-done.2), channel_id=1, replica_groups=mesh['row'=8,'col'=4] {'col'}, dimensions={0}, use_global_device_ids=true | all-gather | bytes 81920 | tf_op jit(solution)/shard_map/all_gather | solution.py:50
  52.9 14.0 %all_gather.24 = bf16[16,4,1024]{2,1,0:T(4,128)(2,1)S(1)} all-gather(bf16[2,4,1024]{2,1,0:T(4,128)(2,1)S(1)} %copy-done.3), channel_id=1, replica_groups=mesh['row'=8,'col'=4] {'row'}, dimensions={0}, use_global_device_ids=true | all-gather | bytes 147456 | tf_op jit(solution)/shard_map/all_gather | solution.py:43
  66.9 7.2 %all_gather.22 = bf16[8,4,1024]{2,1,0:T(4,128)(2,1)S(1)} all-gather(bf16[2,4,1024]{2,1,0:T(4,128)(2,1)S(1)} %copy-done.3), channel_id=1, replica_groups=mesh['row'=8,'col'=4] {'col'}, dimensions={0}, use_global_device_ids=true | all-gather | bytes 81920 | tf_op jit(solution)/shard_map/all_gather | solution.py:49
  75.8 12.8 %all-gather = bf16[8,2,512]{2,1,0:T(2,128)(2,1)S(1)} all-gather(bf16[1,2,512]{2,1,0:T(2,128)(2,1)S(1)} %bitcast.64), channel_id=1, replica_groups=mesh['row'=8,'col'=4] {'row'}, dimensions={0}, use_global_device_ids=true | all-gather | bytes 18432 | tf_op jit(solution)/shard_map/all_gather | solution.py:45
  88.7 33.2 %while.14 = (s32[]{:T(128)}, f32[8,16,32]{2,1,0:T(8,128)S(1)}, bf16[8,16,1024]{2,1,0:T(8,128)(2,1)S(1)}, bf16[16,16,1024]{2,1,0:T(8,128)(2,1)S(1)}, bf16[16,16,3...) while((s32[]{:T(128)}, f32[8,16,32]{2,1,0:T(8,128)S(1)}, ...), condition=%wide.region_2.3_spmd.clone, body=%wide.region_1.2_spmd.clone.sunk | while | flops 14714503 | bytes 2319689 | solution.py:73
  88.7 0.7 constant_dynamic-slice_fusion.2
  91.4 1.1 convolution_bitcast_fusion.8
  92.9 0.7 constant_dynamic-slice_fusion.2
  95.5 1.1 convolution_bitcast_fusion.8
  99.7 1.1 convolution_bitcast_fusion.8
  103.8 1.1 convolution_bitcast_fusion.8
  108.0 1.1 convolution_bitcast_fusion.8
  112.1 1.1 convolution_bitcast_fusion.8
  116.3 1.1 convolution_bitcast_fusion.8
  117.8 0.7 constant_dynamic-slice_fusion.2
  120.4 1.1 convolution_bitcast_fusion.8
  122.8 0.9 convolution_bitcast_fusion.2
  123.7 20.8 %reduce-scatter.4.cloned.1.call-done = f32[1,2,16,32]{3,2,1,0:T(8,128)} async-done(((f32[4,2,16,32]{3,2,1,0:T(8,128)}), f32[1,2,16,32]{3,2,1,0:T(8,128)}) %reduce-scatter.4.cloned.1.call-update) | async-done | bytes 4112
  144.5 105.8 %all-reduce.3.cloned.1.call-done = f32[1024,32]{0,1:T(8,128)} async-done(((f32[1024,32]{0,1:T(8,128)}), f32[1024,32]{0,1:T(8,128)}) %all-reduce.3.cloned.1.call-update) | async-done | bytes 131088 | tf_op jit(solution)/shard_map/psum | solution.py:39
  250.3 1.1 fusion.17
  251.7 39.3 %psum.15 = f32[32,32]{0,1:T(8,128)S(1)} all-reduce(f32[32,32]{0,1:T(8,128)S(1)} %convolution_bitcast_fusion.4), channel_id=1, replica_groups=mesh['row'=8,'col'=4] {'row','col'}, use_global_device_ids=true, to_apply=%region_4.5 | all-reduce | flops 1024 | bytes 8192 | tf_op jit(solution)/shard_map/psum | solution.py:95
  (119 shorter events, 26.9 us)
Async XLA Ops:
  8.0 0.7 copy-start.6
  8.0 136.5 %reduce-scatter.4.cloned.1.call-start = ((), (), s32[]{:S(2)}) async-start(), calls=%async_computation.2 | async-start | bytes 81920
  30.2 14.3 %copy-start.2 = (bf16[2,4,1024]{2,1,0:T(4,128)(2,1)S(1)}, bf16[2,4,1024]{2,1,0:T(4,128)(2,1)}, u32[]{:S(2)}) copy-start(bf16[2,4,1024]{2,1,0:T(4,128)(2,1)} %param.12) | copy-start | bytes 49156
  44.5 8.3 %copy-start.3 = (bf16[2,4,1024]{2,1,0:T(4,128)(2,1)S(1)}, bf16[2,4,1024]{2,1,0:T(4,128)(2,1)}, u32[]{:S(2)}) copy-start(bf16[2,4,1024]{2,1,0:T(4,128)(2,1)} %param.11) | copy-start | bytes 49156
  75.2 0.7 copy-start.4
  121.9 0.6 copy-start
  121.9 0.9 copy-start.1
  122.6 127.7 %all-reduce.3.cloned.1.call-start = ((), (), s32[]{:S(2)}) async-start(), calls=%async_computation.1 | async-start | bytes 262144 | tf_op jit(solution)/shard_map/psum | solution.py:39
  123.7 126.6 %copy-start.5 = (f32[1024]{0:T(1024)S(1)}, f32[1024]{0:T(1024)}, u32[]{:S(2)}) copy-start(f32[1024]{0:T(1024)} %param.13) | copy-start | bytes 12292
  123.7 126.7 %copy-start.7 = (f32[2,16]{1,0:T(2,128)S(1)}, f32[2,16]{1,0:T(2,128)}, u32[]{:S(2)}) copy-start(f32[2,16]{1,0:T(2,128)} %param.15) | copy-start | bytes 388
Sparse Core Ops, SparseCore 0:
  122.7 21.7 reduce-scatter.3
Sparse Core Ops, SparseCore 1:
  128.6 121.7 all-reduce.2
where the time goes:
time: 301 us; the launch traced here: 300 us
  waiting for transfers between devices  127 us (42%)
  blocking collectives  117 us (39%)
  local copies, waits for them, and re-layouts  21.7 us (7%)
  matrix products  16.1 us (5%)
  between operations  15.6 us (5%)
    psum x1, waiting for transfers between devices, on_device(): density = lax.psum(partial_density, ('row', 'col'))  106 us
    psum x1, blocking collectives, on_device(): alpha = lax.psum(gram, ('row', 'col')) / (total_count * band_count)  39.3 us
    unnamed x3, waiting for transfers between devices  20.8 us
    all_gather x1, blocking collectives, on_device(): lax.all_gather(valence, 'row', axis=0, tiled=True)  14.3 us
    all_gather x1, blocking collectives, on_device(): lax.all_gather(conduction, 'row', axis=0, tiled=True)  14 us
    all_gather x1, blocking collectives, on_device(): lax.all_gather(k_coords, 'row', axis=0, tiled=True)  13.5 us
    all_gather x1, blocking collectives, on_device(): lax.all_gather(vectors, 'row', axis=0, tiled=True)  12.8 us
    dot_general x8, matrix products, square_sweep(): jnp.einsum('ijg,jng->ing', coupling, col_proj, precision=highest)  8.7 us
  transfers between devices with their start and end apart: 2, of which 2 were waited for; matrix products, arithmetic and copies ran while one was open for 0% of the time, Pallas kernels for 0%

commit v1 on v0

--- a/solution.py
+++ b/solution.py
@@ -36,7 +36,8 @@
     partial_density = jnp.einsum(
         "ktg,ktn->gn", pair_exchange, moving, preferred_element_type=jnp.float32
     )
-    density = lax.psum(partial_density, ("row", "col"))
+    parts = lax.all_gather(partial_density, ("row", "col"), axis=0, tiled=False)
+    density = parts.sum(axis=0)
     block_size = 128
     sweeps = plane_count // block_size
     col_cond, col_val, col_vec, col_at = (

time: 301 us -> 197 us (0.65)
  waiting for transfers between devices: 127 us -> 16.6 us
  local copies, waits for them, and re-layouts: 21.7 us -> 25.7 us
    psum x1 -> x0, waiting for transfers between devices: 106 us -> none  [on_device(): density = lax.psum(partial_density, ('row', 'col'))]
    unnamed x3, waiting for transfers between devices: 20.8 us -> 16.5 us
    unnamed x21 -> x16, local copies, waits for them, and re-layouts: 2.95 us -> 6.24 us
  transfers between devices with their start and end apart: 2 -> 2, of which waited for: 2 -> 1; matrix products, arithmetic and copies ran while one was open for 0% -> 20% of each run, Pallas kernels for 0% -> 0%
where the time goes in v1:
time: 197 us; the launch traced here: 196 us
  blocking collectives  119 us (60%)
  local copies, waits for them, and re-layouts  25.7 us (13%)
  matrix products  16.7 us (8%)
  waiting for transfers between devices  16.6 us (8%)
  between operations  15.6 us (8%)
  other arithmetic  2.48 us (1%)
    psum x1, blocking collectives, on_device(): alpha = lax.psum(gram, ('row', 'col')) / (total_count * band_count)  39.3 us
    unnamed x3, waiting for transfers between devices  16.5 us
    all_gather x1, blocking collectives, on_device(): lax.all_gather(conduction, 'row', axis=0, tiled=True)  14.5 us
    all_gather x1, blocking collectives, on_device(): lax.all_gather(valence, 'row', axis=0, tiled=True)  14.2 us
    all_gather x1, blocking collectives, on_device(): lax.all_gather(vectors, 'row', axis=0, tiled=True)  12.8 us
    all_gather x1, blocking collectives, on_device(): lax.all_gather(k_coords, 'row', axis=0, tiled=True)  12 us
    all_gather x1, blocking collectives, on_device(): lax.all_gather(conduction, 'col', axis=0, tiled=True)  9.89 us
    dot_general x8, matrix products, square_sweep(): jnp.einsum('ijg,jng->ing', coupling, col_proj, precision=highest)  8.73 us
  transfers between devices with their start and end apart: 2, of which 1 were waited for; matrix products, arithmetic and copies ran while one was open for 20% of the time, Pallas kernels for 0%

profile of v1, /device:TPU:0, one launch (start us, length us, event | category | flops | bytes accessed | tf_op | source)
XLA Modules:
  0.0 196.3 jit_solution(12537116921025192922)
XLA Ops:
  8.1 0.8 reshape.58
  8.8 1.7 convolution_bitcast_fusion.2
  10.6 9.9 %all_gather.30 = bf16[8,4,1024]{2,1,0:T(4,128)(2,1)S(1)} all-gather(bf16[2,4,1024]{2,1,0:T(4,128)(2,1)} %param.11), channel_id=1, replica_groups=mesh['row'=8,'col'=4] {'col'}, dimensions={0}, use_global_device_ids=true | all-gather | bytes 81920 | tf_op jit(solution)/shard_map/all_gather | solution.py:50
  20.5 14.5 %all_gather.32 = bf16[16,4,1024]{2,1,0:T(4,128)(2,1)S(1)} all-gather(bf16[2,4,1024]{2,1,0:T(4,128)(2,1)} %param.11), channel_id=1, replica_groups=mesh['row'=8,'col'=4] {'row'}, dimensions={0}, use_global_device_ids=true | all-gather | bytes 147456 | tf_op jit(solution)/shard_map/all_gather | solution.py:44
  35.0 8.2 %all_gather.29 = bf16[8,4,1024]{2,1,0:T(4,128)(2,1)S(1)} all-gather(bf16[2,4,1024]{2,1,0:T(4,128)(2,1)} %param.12), channel_id=1, replica_groups=mesh['row'=8,'col'=4] {'col'}, dimensions={0}, use_global_device_ids=true | all-gather | bytes 81920 | tf_op jit(solution)/shard_map/all_gather | solution.py:51
  43.3 14.2 %all_gather.31 = bf16[16,4,1024]{2,1,0:T(4,128)(2,1)S(1)} all-gather(bf16[2,4,1024]{2,1,0:T(4,128)(2,1)} %param.12), channel_id=1, replica_groups=mesh['row'=8,'col'=4] {'row'}, dimensions={0}, use_global_device_ids=true | all-gather | bytes 147456 | tf_op jit(solution)/shard_map/all_gather | solution.py:45
  57.5 12.0 %all-gather.3 = s32[8,2,2]{2,1,0:T(2,128)S(1)} all-gather(s32[1,2,2]{2,1,0:T(2,128)} %bitcast.71), channel_id=1, replica_groups=mesh['row'=8,'col'=4] {'row'}, dimensions={0}, use_global_device_ids=true | all-gather | bytes 144 | tf_op jit(solution)/shard_map/all_gather | solution.py:47
  69.6 7.6 %all-gather.2 = s32[4,2,2]{2,1,0:T(2,128)S(1)} all-gather(s32[1,2,2]{2,1,0:T(2,128)} %bitcast.72), channel_id=1, replica_groups=mesh['row'=8,'col'=4] {'col'}, dimensions={0}, use_global_device_ids=true | all-gather | bytes 80 | tf_op jit(solution)/shard_map/all_gather | solution.py:52
  77.8 12.8 %all-gather.1 = bf16[8,2,512]{2,1,0:T(2,128)(2,1)S(1)} all-gather(bf16[1,2,512]{2,1,0:T(2,128)(2,1)S(1)} %bitcast.70), channel_id=1, replica_groups=mesh['row'=8,'col'=4] {'row'}, dimensions={0}, use_global_device_ids=true | all-gather | bytes 18432 | tf_op jit(solution)/shard_map/all_gather | solution.py:46
  91.2 33.2 %while.14 = (s32[]{:T(128)}, f32[8,16,32]{2,1,0:T(8,128)S(1)}, bf16[8,16,1024]{2,1,0:T(8,128)(2,1)S(1)}, bf16[16,16,1024]{2,1,0:T(8,128)(2,1)S(1)}, bf16[16,16,3...) while((s32[]{:T(128)}, f32[8,16,32]{2,1,0:T(8,128)S(1)}, ...), condition=%wide.region_2.3_spmd.clone, body=%wide.region_1.2_spmd.clone.sunk | while | flops 14714503 | bytes 2319697 | solution.py:74
  91.9 0.7 constant_dynamic-slice_fusion.2
  93.8 1.1 convolution_bitcast_fusion.8
  96.1 0.7 constant_dynamic-slice_fusion.2
  98.0 1.1 convolution_bitcast_fusion.8
  102.1 1.1 convolution_bitcast_fusion.8
  106.3 1.1 convolution_bitcast_fusion.8
  110.5 1.1 convolution_bitcast_fusion.8
  114.6 1.1 convolution_bitcast_fusion.8
  118.8 1.1 convolution_bitcast_fusion.8
  122.9 1.1 convolution_bitcast_fusion.8
  125.1 4.6 %copy.33 = f32[4,8,32,1024]{3,2,1,0:T(8,128)S(1)} copy(f32[4,8,32,1024]{3,1,2,0:T(8,128)} %bitcast.62) | data formatting | bytes 8388608
  130.4 16.5 %reduce-scatter.4.cloned.1.call-done = f32[1,2,16,32]{3,2,1,0:T(8,128)} async-done(((f32[4,2,16,32]{3,2,1,0:T(8,128)}), f32[1,2,16,32]{3,2,1,0:T(8,128)}) %reduce-scatter.4.cloned.1.call-update) | async-done | bytes 4112
  146.9 1.0 fusion.17
  148.0 39.3 %psum.7 = f32[32,32]{0,1:T(8,128)S(1)} all-reduce(f32[32,32]{0,1:T(8,128)S(1)} %convolution_bitcast_fusion.4), channel_id=1, replica_groups=mesh['row'=8,'col'=4] {'row','col'}, use_global_device_ids=true, to_apply=%region_4.5 | all-reduce | flops 1024 | bytes 8192 | tf_op jit(solution)/shard_map/psum | solution.py:96
  (115 shorter events, 26.8 us)
Async XLA Ops:
  8.0 69.8 %copy-start.2 = (bf16[2,512]{1,0:T(2,128)(2,1)S(1)}, bf16[2,512]{1,0:T(2,128)(2,1)}, u32[]{:S(2)}) copy-start(bf16[2,512]{1,0:T(2,128)(2,1)} %param.16) | copy-start | bytes 6148
  8.0 117.1 %all-gather.6.cloned.1.call-start = ((), (), s32[]{:S(2)}) async-start(), calls=%async_computation.1 | async-start | bytes 4325376 | tf_op jit(solution)/shard_map/all_gather | solution.py:39
  10.5 136.3 %reduce-scatter.4.cloned.1.call-start = ((), (), s32[]{:S(2)}) async-start(), calls=%async_computation.2 | async-start | bytes 81920
  124.4 0.6 copy-start
  129.7 17.2 %copy-start.1 = (bf16[2,16,1024]{2,1,0:T(8,128)(2,1)S(1)}, bf16[2,16,1024]{2,1,0:T(8,128)(2,1)}, u32[]{:S(2)}) copy-start(bf16[2,16,1024]{2,1,0:T(8,128)(2,1)} %param.10) | copy-start | bytes 196612
  129.7 17.2 %copy-start.3 = (f32[1024]{0:T(1024)S(1)}, f32[1024]{0:T(1024)}, u32[]{:S(2)}) copy-start(f32[1024]{0:T(1024)} %param.13) | copy-start | bytes 12292
  129.7 17.1 %copy-start.4 = (f32[2,16]{1,0:T(2,128)S(1)}, f32[2,16]{1,0:T(2,128)}, u32[]{:S(2)}) copy-start(f32[2,16]{1,0:T(2,128)} %param.15) | copy-start | bytes 388
Sparse Core Ops, SparseCore 0:
  11.7 65.3 all-gather.5
Sparse Core Ops, SparseCore 1:
  125.2 21.7 reduce-scatter.3
